TPU v7x, 32 devices: a whole 2x2x4 slice. The times are simulated.
32 devices in a mesh: occ: 4 (over z), vir: 4 (over y, x), ka: 2 (over core).
Axes of the slice: x: 2, y: 2, z: 4, core: 2. Of those that a mesh axis runs over, the one named last changes fastest.
Arguments:
- lambda_amps: bfloat16 [2, 16, 1024, 1024], P(None, 'occ', 'vir', 'ka'), may hold values from -0.25 to 0.25
- screened_ints: bfloat16 [16, 1024, 1024], P(('occ', 'vir'), 'ka'), may hold values from -6 to 6
- half_ints: bfloat16 [16, 1024, 128], P(('occ', 'vir'), 'ka'), may hold values from -0.5 to 0.5
- singles: bfloat16 [128, 1024], P(None, 'vir'), may hold values from -6 to 6
- block_mask: int32 [16, 8, 8], P('occ', 'ka'), may hold values from 0 to 1, as said below
Outputs:
- residual_part: bfloat16 [2, 16, 1024, 1024], P('ka', 'occ', 'vir')
Inputs may be any that keep to these rules, and one draw needn't show every extreme that they name: `block_mask`: for each j and each of the 2 equal ranges of e blocks, between 1 and 16 of its 32 blocks are 1; some (j, range) has exactly 16.
All inputs are finite; a program needn't handle non-finite values.
Results may differ from a plain program's by a relative error of at most 0.0058.
Values may be sent and summed in bfloat16 or wider, within the bound.
A program may use at most 128 MiB of HBM per device.

v0:
```python
import jax
import jax.numpy as jnp
from jax import lax
from jax.sharding import PartitionSpec as P

TILE = 128


def dense_form(screened_ints, half_ints, single_all, own_mask, tile_size):
    per_vir, half_rows, full_cols = screened_ints.shape
    row_blocks = half_rows // tile_size
    col_blocks = full_cols // tile_size
    dressed = screened_ints.astype(jnp.float32) - jnp.einsum(
        "jem,mb->jeb", half_ints, single_all, preferred_element_type=jnp.float32
    )
    block_gate = own_mask.astype(jnp.float32)[:, :, None, :, None]
    screened = dressed.reshape(per_vir, row_blocks, tile_size, col_blocks, tile_size) * block_gate
    return screened.astype(jnp.bfloat16).reshape(per_vir, half_rows, full_cols)


def body(lambda_amps, screened_ints, half_ints, singles, block_mask):
    tile_size = TILE
    single_all = lax.all_gather(singles, "vir", axis=1, tiled=True)
    per_vir, half_rows, full_cols = screened_ints.shape
    vir_index = lax.axis_index("vir")
    own_mask = lax.dynamic_slice_in_dim(block_mask, vir_index * per_vir, per_vir, 0)
    blocks = dense_form(screened_ints, half_ints, single_all, own_mask, tile_size)
    gathered_w = lax.all_gather(blocks, "vir", axis=0, tiled=True)
    gathered_w = lax.all_gather(gathered_w, "ka", axis=1, tiled=True)
    owned_amps = lax.all_to_all(lambda_amps, "ka", split_axis=0, concat_axis=3, tiled=True)
    owned = jnp.einsum("ijae,jeb->ijab", owned_amps, gathered_w, preferred_element_type=jnp.float32)
    return owned.astype(jnp.bfloat16)


def solution(mesh):
    return jax.shard_map(
        body,
        mesh=mesh,
        in_specs=(
            P(None, "occ", "vir", "ka"),
            P(("occ", "vir"), "ka", None),
            P(("occ", "vir"), "ka", None),
            P(None, "vir"),
            P("occ", "ka", None),
        ),
        out_specs=P("ka", "occ", "vir", None),
        check_vma=False,
    )
```

profile of v0, /device:TPU:1, one launch (start us, length us, event | category | flops | bytes accessed | tf_op | source)
XLA Modules:
  0.0 118.2 jit_solution(17710434797623138036)
XLA Ops:
  6.5 0.0 copy-start
  6.5 0.0 all-gather.3.cloned.1.call-start
  6.5 0.7 convert_bitcast_fusion.1
  7.3 1.5 %mul.16 = f32[4,128,8,128]{3,2,1,0:T(8,128)} broadcast(f32[4,8]{1,0:T(4,128)S(1)} %convert_bitcast_fusion.1), dimensions={0,2} | broadcast | bytes 2097280 | tf_op jit(solution)/shard_map/mul | solution.py:17
  8.8 0.0 copy-start.3
  8.8 0.0 copy-start.2
  8.8 1.8 %mul.17 = f32[1,512,1024]{2,1,0:T(8,128)S(1)} reshape(f32[4,128,8,128]{3,2,1,0:T(8,128)} %mul.16) | data formatting | bytes 4194304 | tf_op jit(solution)/shard_map/mul | solution.py:17
  10.6 0.0 copy-done.3
  10.6 8.8 %all_gather.9 = bf16[128,1024]{1,0:T(8,128)(2,1)S(1)} all-gather(bf16[128,256]{1,0:T(8,128)(2,1)S(1)} %copy-done.3), channel_id=1, replica_groups=mesh['occ'=4,'vir'=4,'ka'=2] {'vir'}, dimensions={1}, use_global_device_ids=true | all-gather | bytes 327680 | tf_op jit(solution)/shard_map/all_gather | solution.py:23
  19.4 0.0 copy-done
  19.5 0.0 copy-done.2
  19.5 1.4 %fusion.1 = bf16[1,512,1024]{2,1,0:T(8,128)(2,1)} fusion(f32[1,512,1024]{2,1,0:T(8,128)S(1)} %mul.17, bf16[1,512,1024]{2,1,0:T(8,128)(2,1)S(1)} %copy-done.2, bf16[128,1024]{1,0:T(8,128)(2,1)S(1)} %all_gather.9, bf16[1,512,128]{2,1,0:T(8,128)(2,1)S(1)} %copy-done), kind=kOutput, calls=%fused_computation.2 | convolution fusion | flops 136314880 | bytes 4587520 | tf_op jit(solution)/shard_map/jem,mb->jeb/dot_general | solution.py:13
  20.8 0.0 all-gather.3.cloned.1.call-update
  20.9 0.0 all-gather.5.cloned.1.call-start
  20.9 54.8 %all-gather.3.cloned.1.call-done = bf16[4,512,1024]{2,1,0:T(8,128)(2,1)} async-done(((bf16[1,512,1024]{2,1,0:T(8,128)(2,1)}), bf16[4,512,1024]{2,1,0:T(8,128)(2,1)}) %all-gather.3.cloned.1.call-update) | async-done | bytes 4194320 | tf_op jit(solution)/shard_map/all_gather | solution.py:28
  75.8 6.3 %copy.9 = bf16[4,512,1024]{1,2,0:T(8,128)(2,1)} copy(bf16[4,512,1024]{2,1,0:T(8,128)(2,1)} %all-gather.3.cloned.1.call-done) | data formatting | bytes 8388608 | tf_op jit(solution)/shard_map/all_gather | solution.py:28
  82.0 0.0 copy-start.1
  82.0 0.0 all-gather.5.cloned.1.call-update
  82.0 1.6 %copy-done.1 = bf16[2,4,256,512]{3,2,1,0:T(8,128)(2,1)S(1)} copy-done((bf16[2,4,256,512]{3,2,1,0:T(8,128)(2,1)S(1)}, bf16[2,4,256,512]{3,2,1,0:T(8,128)(2,1)}, u32[]{:S(2)}) %copy-start.1) | copy-done | bytes 2097176
  83.6 5.9 %all_to_all.15 = bf16[2,4,256,512]{3,2,1,0:T(8,128)(2,1)S(1)} all-to-all(bf16[2,4,256,512]{3,2,1,0:T(8,128)(2,1)S(1)} %copy-done.1), channel_id=1, replica_groups=mesh['occ'=4,'vir'=4,'ka'=2] {'ka'}, dimensions={0} | all-to-all | bytes 4194304 | tf_op jit(solution)/shard_map/all_to_all | solution.py:30
  89.5 2.2 %copy.10 = bf16[1,4,256,2,512]{4,3,2,1,0:T(2,128)(2,1)S(1)} copy(bf16[1,4,256,2,512]{4,2,1,3,0:T(8,128)(2,1)S(1)} %bitcast.23) | data formatting | bytes 4194304 | tf_op jit(solution)/shard_map/all_to_all | solution.py:30
  91.6 2.7 %reshape.23 = bf16[4,256,1024]{2,1,0:T(8,128)(2,1)} reshape(bf16[1,4,256,2,512]{4,3,2,1,0:T(2,128)(2,1)S(1)} %copy.10) | data formatting | bytes 4194304 | tf_op jit(solution)/shard_map/reshape.5
  94.3 8.2 %all-gather.5.cloned.1.call-done = bf16[4,1024,1024]{1,2,0:T(8,128)(2,1)} async-done(((bf16[4,512,1024]{1,2,0:T(8,128)(2,1)}), bf16[4,1024,1024]{1,2,0:T(8,128)(2,1)}) %all-gather.5.cloned.1.call-update) | async-done | bytes 8388624 | tf_op jit(solution)/shard_map/all_gather | solution.py:29
  102.6 6.4 %convert_bitcast_fusion = bf16[1,4,256,1024]{2,3,1,0:T(8,128)(2,1)S(1)} fusion(bf16[4,1024,1024]{1,2,0:T(8,128)(2,1)} %all-gather.5.cloned.1.call-done, bf16[4,256,1024]{2,1,0:T(8,128)(2,1)} %reshape.23), kind=kOutput, calls=%fused_computation.3 | convolution fusion | flops 2148532224 | bytes 12582912 | tf_op jit(solution)/shard_map/ijae,jeb->ijab/dot_general | solution.py:31
  108.9 2.4 %copy.11 = bf16[1,4,256,1024]{3,2,1,0:T(8,128)(2,1)} copy(bf16[1,4,256,1024]{2,3,1,0:T(8,128)(2,1)S(1)} %convert_bitcast_fusion) | data formatting | bytes 4194304 | tf_op jit(solution)/shard_map/convert_element_type | solution.py:32
Async XLA Ops:
  6.5 12.9 %copy-start = (bf16[1,512,128]{2,1,0:T(8,128)(2,1)S(1)}, bf16[1,512,128]{2,1,0:T(8,128)(2,1)}, u32[]{:S(2)}) copy-start(bf16[1,512,128]{2,1,0:T(8,128)(2,1)} %param.7) | copy-start | bytes 393220
  6.5 69.2 %all-gather.3.cloned.1.call-start = ((), (), s32[]{:S(2)}) async-start(), calls=%async_computation.1 | async-start | bytes 5242880 | tf_op jit(solution)/shard_map/all_gather | solution.py:28
  8.8 1.8 %copy-start.3 = (bf16[128,256]{1,0:T(8,128)(2,1)S(1)}, bf16[128,256]{1,0:T(8,128)(2,1)}, u32[]{:S(2)}) copy-start(bf16[128,256]{1,0:T(8,128)(2,1)} %param.8) | copy-start | bytes 196612
  8.8 10.7 %copy-start.2 = (bf16[1,512,1024]{2,1,0:T(8,128)(2,1)S(1)}, bf16[1,512,1024]{2,1,0:T(8,128)(2,1)}, u32[]{:S(2)}) copy-start(bf16[1,512,1024]{2,1,0:T(8,128)(2,1)} %param.6) | copy-start | bytes 3145732
  20.9 81.7 %all-gather.5.cloned.1.call-start = ((), (), s32[]{:S(2)}) async-start(), calls=%async_computation.2 | async-start | bytes 12582912 | tf_op jit(solution)/shard_map/all_gather | solution.py:29
  82.0 1.6 %copy-start.1 = (bf16[2,4,256,512]{3,2,1,0:T(8,128)(2,1)S(1)}, bf16[2,4,256,512]{3,2,1,0:T(8,128)(2,1)}, u32[]{:S(2)}) copy-start(bf16[2,4,256,512]{3,2,1,0:T(8,128)(2,1)} %param.5) | copy-start | bytes 6291460
Sparse Core Ops, SparseCore 0:
  21.0 54.7 all-gather.2
  82.2 20.3 all-gather.4
where the time goes:
time: 119 us; the launch traced here: 118 us
  waiting for transfers between devices  63.1 us (53%)
  local copies, waits for them, and re-layouts  18.4 us (15%)
  blocking collectives  14.7 us (12%)
  between operations  13.4 us (11%)
  matrix products  7.74 us (7%)
    all_gather x1, waiting for transfers between devices, body(): gathered_w = lax.all_gather(blocks, 'vir', axis=0, tiled=True)  54.8 us
    all_gather x1, blocking collectives, body(): single_all = lax.all_gather(singles, 'vir', axis=1, tiled=True)  8.84 us
    all_gather x1, waiting for transfers between devices, body(): gathered_w = lax.all_gather(gathered_w, 'ka', axis=1, tiled=True)  8.25 us
    dot_general x1, matrix products, body(): jnp.einsum('ijae,jeb->ijab', owned_amps, gathered_w, preferred_element_ty...  6.35 us
    all_gather x1, local copies, waits for them, and re-layouts, body(): gathered_w = lax.all_gather(blocks, 'vir', axis=0, tiled=True)  6.26 us
    all_to_all x1, blocking collectives, body(): lax.all_to_all(lambda_amps, 'ka', split_axis=0, concat_axis=3, tiled=True)  5.87 us
    mul x2, local copies, waits for them, and re-layouts, dense_form(): dressed.reshape(per_vir, row_blocks, tile_size, col_blocks, tile_size)  3.33 us
    another operation x1, local copies, waits for them, and re-layouts  2.71 us
  transfers between devices with their start and end apart: 2, of which 2 were waited for; matrix products, arithmetic and copies ran while one was open for 4% of the time, Pallas kernels for 0%

commit v1 on v0

v1 whole, which is shorter than its diff:
```python
import functools

import jax
import jax.numpy as jnp
from jax import lax
from jax.experimental import pallas as pl
from jax.experimental.pallas import tpu as pltpu
from jax.sharding import PartitionSpec as P

TILE = 128
CAP = 16
CHUNKS = 4


def peers_of(v, n, grid):
    if grid:
        y, x = v // 2, v % 2
        ids = [v, y * 2 + (1 - x), (1 - y) * 2 + x, (1 - y) * 2 + (1 - x)]
        return ids, ids
    return [(v + k) % n for k in range(n)], [(v + n - k) % n for k in range(n)]


def kernel(n, lam, x, y, t, mask, out, lam_v, x_v, y_v, dressed, dense, own, give, take, res, following,
           in_sem, t_send, t_recv, b_send, b_recv, f_send, p_send, p_recv, o_sem, *bufs):
    t_v, gath = bufs[:n], bufs[n:]
    grid = n == 4
    v, c = lax.axis_index("vir"), lax.axis_index("ka")
    dst, src = peers_of(v, n, grid)
    partner = 1 - c
    half = x_v.shape[0]
    width = t_v[0].shape[1]
    cols = width // TILE
    row_blocks = half // TILE
    col_blocks = x_v.shape[1] // TILE
    blocks = row_blocks * col_blocks
    per = CAP // CHUNKS

    loads = [
        pltpu.make_async_copy(t, t_v[0], in_sem.at[0]),
        pltpu.make_async_copy(y.at[0], y_v, in_sem.at[1]),
        pltpu.make_async_copy(x.at[0], x_v, in_sem.at[2]),
        pltpu.make_async_copy(lam, lam_v, in_sem.at[3]),
    ]
    for load in loads:
        load.start()

    barrier = pltpu.get_barrier_semaphore()
    for k in range(1, n):
        pl.semaphore_signal(barrier, inc=1, device_id={"vir": dst[k]}, device_id_type=pl.DeviceIdType.MESH)
    pl.semaphore_signal(barrier, inc=1, device_id={"ka": partner}, device_id_type=pl.DeviceIdType.MESH)
    loads[0].wait()
    pl.semaphore_wait(barrier, n)

    def remote(source, target, send, recv, where):
        return pltpu.make_async_remote_copy(
            src_ref=source, dst_ref=target, send_sem=send, recv_sem=recv,
            device_id=where, device_id_type=pl.DeviceIdType.MESH)

    t_copies = [None] + [
        remote(t_v[0], t_v[k], t_send.at[k], t_recv.at[k], {"vir": dst[k]}) for k in range(1, n)]
    for copy in t_copies[1:]:
        copy.start()

    following[blocks] = blocks - 1
    later = jnp.int32(blocks - 1)
    for p in reversed(range(blocks)):
        later = jnp.where(mask[v, p // col_blocks, p % col_blocks] != 0, p, later)
        following[p] = later

    loads[1].wait()
    loads[2].wait()

    for k in range(n):
        if k:
            t_copies[k].wait_recv()
        start = src[k] * width
        term = jnp.dot(y_v[...], t_v[k][...], preferred_element_type=jnp.float32)
        part = (x_v[:, pl.ds(pl.multiple_of(start, TILE), width)].astype(jnp.float32) - term).astype(jnp.bfloat16)
        for e in range(row_blocks):
            for b in range(cols):
                dressed[e * col_blocks + src[k] * cols + b] = part[e * TILE:(e + 1) * TILE, b * TILE:(b + 1) * TILE]

    def chunk(ref, q):
        return ref.at[pl.ds(q * per, per)]

    def own_copy(k, q):
        return remote(chunk(gath[0], q), chunk(gath[k], q), b_send.at[k, q], b_recv.at[k, q], {"vir": dst[k]})

    def relay_copy(k, q):
        return remote(chunk(gath[k], q), chunk(gath[3], q), f_send.at[q], b_recv.at[3, q], {"vir": dst[3 - k]})

    direct = (1, 2) if grid else tuple(range(1, n))
    relays = [(1, q) for q in range(CHUNKS // 2)] + [(2, q) for q in range(CHUNKS // 2, CHUNKS)]
    place = jnp.int32(-1)
    order = []
    for s in range(CAP):
        place = following[jnp.minimum(place + 1, blocks)]
        order.append(place)
    halves = (list(range(CHUNKS // 2)), list(range(CHUNKS // 2, CHUNKS)))
    for low, high in zip(*halves):
        for q in (low, high):
            for s in range(q * per, (q + 1) * per):
                gath[0][s] = dressed[order[s]]
        if grid:
            own_copy(1, low).start()
            own_copy(2, high).start()
    if grid:
        for low, high in zip(*halves):
            own_copy(1, high).start()
            own_copy(2, low).start()
    else:
        for k in direct:
            for q in range(CHUNKS):
                own_copy(k, q).start()

    def partner_copy(j, k):
        return remote(give.at[k], take.at[k], p_send.at[k], p_recv.at[k], {"ka": partner})

    def form(k):
        j = src[k]

        def rows(e, count):
            for b in range(col_blocks):
                live = mask[j, e, b]
                block = gath[k][jnp.minimum(count, CAP - 1)]
                dense[pl.ds(pl.multiple_of(e * TILE, TILE), TILE), b * TILE:(b + 1) * TILE] = jnp.where(
                    live != 0, block, jnp.zeros_like(block))
                count = count + live
            return count

        lax.fori_loop(0, row_blocks, rows, jnp.int32(0))
        give[k] = jnp.dot(lam_v[partner, j], dense[...], preferred_element_type=jnp.float32).astype(jnp.bfloat16)
        own[k] = jnp.dot(lam_v[c, j], dense[...], preferred_element_type=jnp.float32)
        partner_copy(j, k).start()

    def out_copy(k):
        return pltpu.make_async_copy(res.at[k], out.at[0, src[k]], o_sem.at[k])

    def finish(k):
        partner_copy(src[k], k).wait_recv()
        res[k] = (own[k] + take[k].astype(jnp.float32)).astype(jnp.bfloat16)
        out_copy(k).start()

    loads[3].wait()
    form(0)
    if grid:
        for k, q in relays:
            own_copy(k, q).wait_recv()
            relay_copy(k, q).start()
        done = set(relays)
    else:
        done = set()
    for k in range(1, n):
        for q in range(CHUNKS):
            if (k, q) not in done:
                own_copy(k, q).wait_recv()
        form(k)
        finish(k - 1)
    finish(n - 1)

    for k in range(1, n):
        t_copies[k].wait_send()
    for k in direct:
        for q in range(CHUNKS):
            own_copy(k, q).wait_send()
    if grid:
        for k, q in relays:
            relay_copy(k, q).wait_send()
    for k in range(n):
        partner_copy(src[k], k).wait_send()
        out_copy(k).wait()


def body(n, lambda_amps, screened_ints, half_ints, singles, block_mask):
    wide, pairs, rows, half = lambda_amps.shape
    full = screened_ints.shape[2]
    inner, width = singles.shape
    blocks = (half // TILE) * (full // TILE)
    bf16, f32 = jnp.bfloat16, jnp.float32
    dma = pltpu.SemaphoreType.DMA
    anywhere = pl.BlockSpec(memory_space=pl.ANY)
    return pl.pallas_call(
        functools.partial(kernel, n),
        out_shape=jax.ShapeDtypeStruct((1, pairs, rows, full), bf16),
        in_specs=[anywhere] * 4 + [pl.BlockSpec(memory_space=pltpu.SMEM)],
        out_specs=anywhere,
        scratch_shapes=[
            pltpu.VMEM(lambda_amps.shape, bf16),
            pltpu.VMEM((half, full), bf16),
            pltpu.VMEM((half, inner), bf16),
            pltpu.VMEM((blocks, TILE, TILE), bf16),
            pltpu.VMEM((half, full), bf16),
            pltpu.VMEM((n, rows, full), f32),
            pltpu.VMEM((n, rows, full), bf16),
            pltpu.VMEM((n, rows, full), bf16),
            pltpu.VMEM((n, rows, full), bf16),
            pltpu.SMEM((blocks + 1,), jnp.int32),
            dma((4,)), dma((n,)), dma((n,)), dma((n, CHUNKS)), dma((n, CHUNKS)), dma((CHUNKS,)),
            dma((n,)), dma((n,)), dma((n,)),
        ] + [pltpu.VMEM((inner, width), bf16)] * n + [pltpu.VMEM((CAP, TILE, TILE), bf16)] * n,
        compiler_params=pltpu.CompilerParams(
            collective_id=0, has_side_effects=True, vmem_limit_bytes=56 * 1024 * 1024),
    )(lambda_amps, screened_ints, half_ints, singles, block_mask)


def solution(mesh):
    return jax.shard_map(
        functools.partial(body, mesh.shape["vir"]),
        mesh=mesh,
        in_specs=(
            P(None, "occ", "vir", "ka"),
            P(("occ", "vir"), "ka", None),
            P(("occ", "vir"), "ka", None),
            P(None, "vir"),
            P("occ", "ka", None),
        ),
        out_specs=P("ka", "occ", "vir", None),
        check_vma=False,
    )
```

time: 119 us -> 33.9 us (0.28)
  waiting for transfers between devices: 63.1 us -> 0 us
  Pallas kernels: 0 us -> 30.6 us
  local copies, waits for them, and re-layouts: 18.4 us -> 3.08 us
  blocking collectives: 14.7 us -> 0 us
  between operations: 13.4 us -> 0.01 us
  matrix products: 7.74 us -> 0 us
    all_gather x2 -> x0, waiting for transfers between devices: 63.1 us -> none  [the longest x1 54.8 us: body(): gathered_w = lax.all_gather(blocks, 'vir', axis=0, tiled=True)]
    pallas_call x0 -> x1, Pallas kernels: none -> 30.6 us  [body(): pl.pallas_call(functools.partial(kernel, n), out_shape=jax.ShapeDtypeStru...]
    all_gather x1 -> x0, blocking collectives: 8.84 us -> none  [body(): single_all = lax.all_gather(singles, 'vir', axis=1, tiled=True)]
    dot_general x2 -> x0, matrix products: 7.74 us -> none  [the longest x1 6.35 us: body(): jnp.einsum('ijae,jeb->ijab', owned_amps, gathered_w, preferred_element_ty...]
    all_gather x1 -> x0, local copies, waits for them, and re-layouts: 6.26 us -> none  [body(): gathered_w = lax.all_gather(blocks, 'vir', axis=0, tiled=True)]
    all_to_all x1 -> x0, blocking collectives: 5.87 us -> none  [body(): lax.all_to_all(lambda_amps, 'ka', split_axis=0, concat_axis=3, tiled=True)]
    mul x2 -> x0, local copies, waits for them, and re-layouts: 3.33 us -> none  [dense_form(): dressed.reshape(per_vir, row_blocks, tile_size, col_blocks, tile_size)]
    another operation x1 -> x0, local copies, waits for them, and re-layouts: 2.71 us -> none
  transfers between devices with their start and end apart: 2 -> 0, of which waited for: 2 -> 0; matrix products, arithmetic and copies ran while one was open for 4% -> 0% of each run, Pallas kernels for 0% -> 0%
where the time goes in v1:
time: 33.9 us; the launch traced here: 33.7 us
  Pallas kernels  30.6 us (90%)
  local copies, waits for them, and re-layouts  3.08 us (9%)
    pallas_call x1, Pallas kernels, body(): pl.pallas_call(functools.partial(kernel, n), out_shape=jax.ShapeDtypeStru...  30.6 us
    unnamed x1, local copies, waits for them, and re-layouts  3.08 us

profile of v1, /device:TPU:1, one launch (start us, length us, event | category | flops | bytes accessed | tf_op | source)
XLA Modules:
  0.0 33.7 jit_solution(12362016865699352988)
XLA Ops:
  0.0 30.6 %shard_map.55 = bf16[1,4,256,1024]{3,2,1,0:T(8,128)(2,1)} custom-call(bf16[2,4,256,512]{3,2,1,0:T(8,128)(2,1)} %lam.1, bf16[1,512,1024]{2,1,0:T(8,128)(2,1)} %x.1, bf16[1,512,128]{2,1,0:T(8,128)(2,1)} %y.1, bf16[128,256]{1,0:T(8,128)(2,1)} %t.1, s32[4,4,8]{2,1,0:T(4,128)} %mask.1), custom_call_target="tpu_custom_call" | custom-call | tf_op jit(solution)/shard_map/pallas_call | solution.py:182
  30.6 3.1 %copy.7 = bf16[1,4,256,1024]{3,2,1,0:T(8,128)(2,1)} copy(bf16[1,4,256,1024]{3,2,1,0:T(8,128)(2,1)} %shard_map.55) | data formatting | bytes 4194304

commit v2 on v1

--- a/solution.py
+++ b/solution.py
@@ -9,6 +9,7 @@
 
 TILE = 128
 CAP = 16
+SIDES = 2
 CHUNKS = 4
 
 
@@ -20,8 +21,8 @@
     return [(v + k) % n for k in range(n)], [(v + n - k) % n for k in range(n)]
 
 
-def kernel(n, lam, x, y, t, mask, out, lam_v, x_v, y_v, dressed, dense, own, give, take, res, following,
-           in_sem, t_send, t_recv, b_send, b_recv, f_send, p_send, p_recv, o_sem, *bufs):
+def kernel(n, lam, x, y, t, mask, out, lam_v, x_v, y_v, dressed, dense, own, give, take, following,
+           in_sem, t_send, t_recv, h_send, h_recv, b_send, b_recv, f_send, p_send, p_recv, *bufs):
     t_v, gath = bufs[:n], bufs[n:]
     grid = n == 4
     v, c = lax.axis_index("vir"), lax.axis_index("ka")
@@ -56,9 +57,15 @@
             src_ref=source, dst_ref=target, send_sem=send, recv_sem=recv,
             device_id=where, device_id_type=pl.DeviceIdType.MESH)
 
+    share = t_v[0].shape[0] // 2
+    part_rows = pl.ds(pl.multiple_of(c * share, share), share)
     t_copies = [None] + [
-        remote(t_v[0], t_v[k], t_send.at[k], t_recv.at[k], {"vir": dst[k]}) for k in range(1, n)]
-    for copy in t_copies[1:]:
+        remote(t_v[0].at[part_rows], t_v[k].at[part_rows], t_send.at[k], t_recv.at[k], {"vir": dst[k]})
+        for k in range(1, n)]
+    t_swaps = [None] + [
+        remote(t_v[k].at[part_rows], t_v[k].at[part_rows], h_send.at[k], h_recv.at[k], {"ka": partner})
+        for k in range(1, n)]
+    for copy in reversed(t_copies[1:]):
         copy.start()
 
     following[blocks] = blocks - 1
@@ -70,15 +77,21 @@
     loads[1].wait()
     loads[2].wait()
 
-    for k in range(n):
-        if k:
-            t_copies[k].wait_recv()
+    def dress(k):
         start = src[k] * width
         term = jnp.dot(y_v[...], t_v[k][...], preferred_element_type=jnp.float32)
         part = (x_v[:, pl.ds(pl.multiple_of(start, TILE), width)].astype(jnp.float32) - term).astype(jnp.bfloat16)
         for e in range(row_blocks):
             for b in range(cols):
                 dressed[e * col_blocks + src[k] * cols + b] = part[e * TILE:(e + 1) * TILE, b * TILE:(b + 1) * TILE]
+
+    dress(0)
+    for k in range(1, n):
+        t_copies[k].wait_recv()
+        t_swaps[k].start()
+    for k in range(1, n):
+        t_swaps[k].wait_recv()
+        dress(k)
 
     def chunk(ref, q):
         return ref.at[pl.ds(q * per, per)]
@@ -113,8 +126,11 @@
             for q in range(CHUNKS):
                 own_copy(k, q).start()
 
-    def partner_copy(j, k):
-        return remote(give.at[k], take.at[k], p_send.at[k], p_recv.at[k], {"ka": partner})
+    side = x_v.shape[1] // SIDES
+
+    def partner_copy(k, h):
+        columns = pl.ds(h * side, side)
+        return remote(give.at[k, :, columns], take.at[k, :, columns], p_send.at[k, h], p_recv.at[k, h], {"ka": partner})
 
     def form(k):
         j = src[k]
@@ -129,17 +145,19 @@
             return count
 
         lax.fori_loop(0, row_blocks, rows, jnp.int32(0))
-        give[k] = jnp.dot(lam_v[partner, j], dense[...], preferred_element_type=jnp.float32).astype(jnp.bfloat16)
+        for h in range(SIDES):
+            columns = slice(h * side, (h + 1) * side)
+            give[k, :, columns] = jnp.dot(
+                lam_v[partner, j], dense[:, columns], preferred_element_type=jnp.float32).astype(jnp.bfloat16)
+            partner_copy(k, h).start()
         own[k] = jnp.dot(lam_v[c, j], dense[...], preferred_element_type=jnp.float32)
-        partner_copy(j, k).start()
-
-    def out_copy(k):
-        return pltpu.make_async_copy(res.at[k], out.at[0, src[k]], o_sem.at[k])
 
     def finish(k):
-        partner_copy(src[k], k).wait_recv()
-        res[k] = (own[k] + take[k].astype(jnp.float32)).astype(jnp.bfloat16)
-        out_copy(k).start()
+        for h in range(SIDES):
+            columns = slice(h * side, (h + 1) * side)
+            partner_copy(k, h).wait_recv()
+            out[0, src[k], :, columns] = (
+                own[k, :, columns] + take[k, :, columns].astype(jnp.float32)).astype(jnp.bfloat16)
 
     loads[3].wait()
     form(0)
@@ -160,6 +178,7 @@
 
     for k in range(1, n):
         t_copies[k].wait_send()
+        t_swaps[k].wait_send()
     for k in direct:
         for q in range(CHUNKS):
             own_copy(k, q).wait_send()
@@ -167,8 +186,8 @@
         for k, q in relays:
             relay_copy(k, q).wait_send()
     for k in range(n):
-        partner_copy(src[k], k).wait_send()
-        out_copy(k).wait()
+        for h in range(SIDES):
+            partner_copy(k, h).wait_send()
 
 
 def body(n, lambda_amps, screened_ints, half_ints, singles, block_mask):
@@ -181,9 +200,9 @@
     anywhere = pl.BlockSpec(memory_space=pl.ANY)
     return pl.pallas_call(
         functools.partial(kernel, n),
-        out_shape=jax.ShapeDtypeStruct((1, pairs, rows, full), bf16),
+        out_shape=pltpu.VMEM((1, pairs, rows, full), bf16),
         in_specs=[anywhere] * 4 + [pl.BlockSpec(memory_space=pltpu.SMEM)],
-        out_specs=anywhere,
+        out_specs=pl.BlockSpec(memory_space=pltpu.VMEM),
         scratch_shapes=[
             pltpu.VMEM(lambda_amps.shape, bf16),
             pltpu.VMEM((half, full), bf16),
@@ -193,10 +212,9 @@
             pltpu.VMEM((n, rows, full), f32),
             pltpu.VMEM((n, rows, full), bf16),
             pltpu.VMEM((n, rows, full), bf16),
-            pltpu.VMEM((n, rows, full), bf16),
             pltpu.SMEM((blocks + 1,), jnp.int32),
-            dma((4,)), dma((n,)), dma((n,)), dma((n, CHUNKS)), dma((n, CHUNKS)), dma((CHUNKS,)),
-            dma((n,)), dma((n,)), dma((n,)),
+            dma((4,)), dma((n,)), dma((n,)), dma((n,)), dma((n,)), dma((n, CHUNKS)), dma((n, CHUNKS)), dma((CHUNKS,)),
+            dma((n, SIDES)), dma((n, SIDES)),
         ] + [pltpu.VMEM((inner, width), bf16)] * n + [pltpu.VMEM((CAP, TILE, TILE), bf16)] * n,
         compiler_params=pltpu.CompilerParams(
             collective_id=0, has_side_effects=True, vmem_limit_bytes=56 * 1024 * 1024),

time: 33.9 us -> 32.4 us (0.956)
  local copies, waits for them, and re-layouts: 3.08 us -> 1.32 us
    unnamed x1, local copies, waits for them, and re-layouts: 3.08 us -> 1.32 us
where the time goes in v2:
time: 32.4 us; the launch traced here: 32.1 us
  Pallas kernels  30.8 us (95%)
  local copies, waits for them, and re-layouts  1.32 us (4%)
    pallas_call x1, Pallas kernels, body(): pl.pallas_call(functools.partial(kernel, n), out_shape=pltpu.VMEM((1, pai...  30.8 us
    unnamed x1, local copies, waits for them, and re-layouts  1.32 us

profile of v2, /device:TPU:1, one launch (start us, length us, event | category | flops | bytes accessed | tf_op | source)
XLA Modules:
  0.0 32.1 jit_solution(7534408320995341045)
XLA Ops:
  0.0 30.8 %shard_map.55 = bf16[1,4,256,1024]{3,2,1,0:T(8,128)(2,1)S(1)} custom-call(bf16[2,4,256,512]{3,2,1,0:T(8,128)(2,1)} %lam.1, bf16[1,512,1024]{2,1,0:T(8,128)(2,1)} %x.1, bf16[1,512,128]{2,1,0:T(8,128)(2,1)} %y.1, bf16[128,256]{1,0:T(8,128)(2,1)} %t.1, s32[4,4,8]{2,1,0:T(4,128)} %mask.1), custom_call_target="tpu_custom_call" | custom-call | tf_op jit(solution)/shard_map/pallas_call | solution.py:201
  30.8 1.3 %copy.7 = bf16[1,4,256,1024]{3,2,1,0:T(8,128)(2,1)} copy(bf16[1,4,256,1024]{3,2,1,0:T(8,128)(2,1)S(1)} %shard_map.55) | data formatting | bytes 4194304

commit v3 on v2

--- a/solution.py
+++ b/solution.py
@@ -10,7 +10,7 @@
 TILE = 128
 CAP = 16
 SIDES = 2
-CHUNKS = 4
+CHUNKS = 2
 
 
 def peers_of(v, n, grid):
@@ -22,7 +22,7 @@
 
 
 def kernel(n, lam, x, y, t, mask, out, lam_v, x_v, y_v, dressed, dense, own, give, take, following,
-           in_sem, t_send, t_recv, h_send, h_recv, b_send, b_recv, f_send, p_send, p_recv, *bufs):
+           in_sem, t_send, t_recv, b_send, b_recv, f_send, p_send, p_recv, *bufs):
     t_v, gath = bufs[:n], bufs[n:]
     grid = n == 4
     v, c = lax.axis_index("vir"), lax.axis_index("ka")
@@ -57,13 +57,8 @@
             src_ref=source, dst_ref=target, send_sem=send, recv_sem=recv,
             device_id=where, device_id_type=pl.DeviceIdType.MESH)
 
-    share = t_v[0].shape[0] // 2
-    part_rows = pl.ds(pl.multiple_of(c * share, share), share)
     t_copies = [None] + [
-        remote(t_v[0].at[part_rows], t_v[k].at[part_rows], t_send.at[k], t_recv.at[k], {"vir": dst[k]})
-        for k in range(1, n)]
-    t_swaps = [None] + [
-        remote(t_v[k].at[part_rows], t_v[k].at[part_rows], h_send.at[k], h_recv.at[k], {"ka": partner})
+        remote(t_v[0], t_v[k], t_send.at[k], t_recv.at[k], {"vir": dst[k]})
         for k in range(1, n)]
     for copy in reversed(t_copies[1:]):
         copy.start()
@@ -88,9 +83,7 @@
     dress(0)
     for k in range(1, n):
         t_copies[k].wait_recv()
-        t_swaps[k].start()
-    for k in range(1, n):
-        t_swaps[k].wait_recv()
+    for k in range(1, n):
         dress(k)
 
     def chunk(ref, q):
@@ -169,16 +162,18 @@
     else:
         done = set()
     for k in range(1, n):
+        if k == n - 1:
+            finish(k - 1)
         for q in range(CHUNKS):
             if (k, q) not in done:
                 own_copy(k, q).wait_recv()
         form(k)
-        finish(k - 1)
+        if k < n - 1:
+            finish(k - 1)
     finish(n - 1)
 
     for k in range(1, n):
         t_copies[k].wait_send()
-        t_swaps[k].wait_send()
     for k in direct:
         for q in range(CHUNKS):
             own_copy(k, q).wait_send()
@@ -213,7 +208,7 @@
             pltpu.VMEM((n, rows, full), bf16),
             pltpu.VMEM((n, rows, full), bf16),
             pltpu.SMEM((blocks + 1,), jnp.int32),
-            dma((4,)), dma((n,)), dma((n,)), dma((n,)), dma((n,)), dma((n, CHUNKS)), dma((n, CHUNKS)), dma((CHUNKS,)),
+            dma((4,)), dma((n,)), dma((n,)), dma((n, CHUNKS)), dma((n, CHUNKS)), dma((CHUNKS,)),
             dma((n, SIDES)), dma((n, SIDES)),
         ] + [pltpu.VMEM((inner, width), bf16)] * n + [pltpu.VMEM((CAP, TILE, TILE), bf16)] * n,
         compiler_params=pltpu.CompilerParams(

time: 32.4 us -> 32 us (0.988)
  Pallas kernels: 30.8 us -> 30.4 us
    pallas_call x1, Pallas kernels: 30.8 us -> 30.4 us  [body(): pl.pallas_call(functools.partial(kernel, n), out_shape=pltpu.VMEM((1, pai...]
where the time goes in v3:
time: 32 us; the launch traced here: 31.7 us
  Pallas kernels  30.4 us (95%)
  local copies, waits for them, and re-layouts  1.32 us (4%)
    pallas_call x1, Pallas kernels, body(): pl.pallas_call(functools.partial(kernel, n), out_shape=pltpu.VMEM((1, pai...  30.4 us
    unnamed x1, local copies, waits for them, and re-layouts  1.32 us

profile of v3, /device:TPU:1, one launch (start us, length us, event | category | flops | bytes accessed | tf_op | source)
XLA Modules:
  0.0 31.7 jit_solution(17494348974973422500)
XLA Ops:
  0.0 30.4 %shard_map.55 = bf16[1,4,256,1024]{3,2,1,0:T(8,128)(2,1)S(1)} custom-call(bf16[2,4,256,512]{3,2,1,0:T(8,128)(2,1)} %lam.1, bf16[1,512,1024]{2,1,0:T(8,128)(2,1)} %x.1, bf16[1,512,128]{2,1,0:T(8,128)(2,1)} %y.1, bf16[128,256]{1,0:T(8,128)(2,1)} %t.1, s32[4,4,8]{2,1,0:T(4,128)} %mask.1), custom_call_target="tpu_custom_call" | custom-call | tf_op jit(solution)/shard_map/pallas_call | solution.py:196
  30.4 1.3 %copy.7 = bf16[1,4,256,1024]{3,2,1,0:T(8,128)(2,1)} copy(bf16[1,4,256,1024]{3,2,1,0:T(8,128)(2,1)S(1)} %shard_map.55) | data formatting | bytes 4194304
